TPU v7x, 256 devices: a whole 4x4x8 slice. The times are simulated.
256 devices in a mesh: row: 8 (over y, x_lo), col: 32 (over z, x_hi, core).
Axes of the slice: x: 4 (x_hi: 2, x_lo: 2; x = x_hi * 2 + x_lo), y: 4, z: 8, core: 2. Of those that a mesh axis runs over, the one named last changes fastest.
Arguments:
- pair_rep: bfloat16 [1024, 1024, 128], P('row', 'col'), may hold values from -6 to 6
- proj_weight: bfloat16 [2, 4, 128, 128], replicated, may hold values from -0.5 to 0.5
- gate_weight: bfloat16 [2, 128, 128], replicated, may hold values from -0.5 to 0.5
- out_weight: bfloat16 [2, 128, 128], replicated, may hold values from -0.5 to 0.5
- in_gain: float32 [2, 128], replicated, may hold values from 0.1 to 1.9
- out_gain: float32 [2, 128], replicated, may hold values from 0.1 to 1.9
Outputs:
- updated_pair: bfloat16 [1024, 1024, 128], P('row', 'col')
All inputs are finite; a program needn't handle non-finite values.
Results may differ from a plain program's by a relative error of at most 0.011.
Values may be sent and summed in bfloat16 or wider, within the bound.
No kernel may reach another device: no remote copies, remote signals or barrier semaphores. Data moves between devices by JAX's collectives and lax.ppermute only.
A program may use at most 64 MiB of HBM per device.

v0:
```python
import jax
import jax.numpy as jnp
from jax import lax
from jax.sharding import Mesh
from jax.sharding import PartitionSpec as P

ROW = ("row_0", "row_1")
epsilon = 1e-05


def sum_by_axis(terms, axes):
    subtotal = terms.astype(jnp.bfloat16)
    for axis in axes:
        subtotal = lax.psum_scatter(subtotal, axis, scatter_dimension=0, tiled=True)
    return subtotal.astype(jnp.float32)


def layer_norm(values, gain_row, reduce_axis):
    center = values - jnp.mean(values, axis=reduce_axis, keepdims=True)
    spread = jnp.mean(center * center, axis=reduce_axis, keepdims=True)
    return center * lax.rsqrt(spread + epsilon) * gain_row


def local(pair_rep, proj_weight, gate_weight, out_weight, in_gain, out_gain):
    current = pair_rep
    for update_index in range(2):
        widened = current.astype(jnp.float32)
        normed = layer_norm(widened, in_gain[update_index], 2).astype(jnp.bfloat16)
        projected = jnp.einsum(
            "ijc,pch->phij", normed, proj_weight[update_index], preferred_element_type=jnp.float32
        )
        left_hand = (jax.nn.sigmoid(projected[0]) * projected[1]).astype(jnp.bfloat16)
        right_hand = (jax.nn.sigmoid(projected[2]) * projected[3]).astype(jnp.bfloat16)
        gating = jax.nn.sigmoid(
            jnp.dot(normed, gate_weight[update_index], preferred_element_type=jnp.float32)
        )
        left_rows, right_rows = (
            lax.all_to_all(left_hand, "col", split_axis=0, concat_axis=2, tiled=True),
            lax.all_to_all(right_hand, "col", split_axis=0, concat_axis=2, tiled=True),
        )
        if update_index == 0:
            triangle = jnp.einsum(
                "gik,gjk->igj",
                left_rows,
                lax.all_gather(right_rows, ROW, axis=1, tiled=True),
                preferred_element_type=jnp.float32,
            )
        else:
            triangle = sum_by_axis(
                jnp.einsum(
                    "gki,gkj->igj", left_rows, right_rows, preferred_element_type=jnp.float32
                ),
                ROW,
            )
        returned = lax.all_to_all(
            triangle.astype(jnp.bfloat16), "col", split_axis=2, concat_axis=1, tiled=True
        )
        mixed_rows = layer_norm(
            returned.astype(jnp.float32), out_gain[update_index][None, :, None], 1
        ).astype(jnp.bfloat16)
        update = jnp.einsum(
            "ihj,hc->ijc", mixed_rows, out_weight[update_index], preferred_element_type=jnp.float32
        )
        current = (widened + gating * update).astype(jnp.bfloat16)
    return current


def solution(mesh):
    finer = Mesh(mesh.devices.reshape(4, 2, mesh.shape["col"]), ("row_0", "row_1", "col"))
    placed = (P(ROW, "col", None), P(), P(), P(), P(), P())
    return jax.shard_map(
        local, mesh=finer, in_specs=placed, out_specs=P(ROW, "col", None), check_vma=False
    )
```

profile of v0, /device:TPU:4, one launch (start us, length us, event | category | flops | bytes accessed | tf_op | source)
XLA Modules:
  0.0 535.5 jit_solution(13058157798516220307)
XLA Ops:
  6.5 2.0 copy.75
  11.6 1.7 copy.79
  13.3 40.5 %all_to_all.90 = bf16[128,128,32]{1,2,0:T(8,128)(2,1)S(1)} all-to-all(bf16[128,128,32]{1,2,0:T(8,128)(2,1)} %copy.79), channel_id=1, replica_groups=mesh['row_0'=4,'row_1'=2,'col'=32] {'col'}, dimensions={0} | all-to-all | bytes 2097152 | tf_op jit(solution)/shard_map/all_to_all | solution.py:39
  56.2 33.7 %all_to_all.91 = bf16[128,128,32]{1,2,0:T(8,128)(2,1)S(1)} all-to-all(bf16[128,128,32]{1,2,0:T(8,128)(2,1)S(1)} %copy.82), channel_id=1, replica_groups=mesh['row_0'=4,'row_1'=2,'col'=32] {'col'}, dimensions={0} | all-to-all | bytes 2097152 | tf_op jit(solution)/shard_map/all_to_all | solution.py:38
  90.0 142.3 %all-gather.2.cloned.1.call-done = bf16[4,1024,1024]{2,1,0:T(8,128)(2,1)} async-done(((bf16[4,128,1024]{2,1,0:T(8,128)(2,1)}), bf16[4,1024,1024]{2,1,0:T(8,128)(2,1)}) %all-gather.2.cloned.1.call-update) | async-done | bytes 8388624 | tf_op jit(solution)/shard_map/all_gather | solution.py:45
  232.4 5.7 %fusion.42 = bf16[128,4,1024]{0,2,1:T(8,128)(2,1)S(1)} fusion(bf16[4,1024,1024]{2,1,0:T(8,128)(2,1)} %all-gather.2.cloned.1.call-done, bf16[4,128,1024]{1,2,0:T(8,128)(2,1)S(1)} %bitcast.134), kind=kOutput, calls=%fused_computation.62 | convolution fusion | flops 1074266112 | bytes 10485760 | tf_op jit(solution)/shard_map/gik,gjk->igj/dot_general | solution.py:42
  238.1 1.8 copy.85
  239.9 9.8 %all-to-all-start.2 = ((bf16[128,4,1024]{0,1,2:T(4,128)(2,1)}), bf16[128,4,1024]{0,1,2:T(4,128)(2,1)S(1)}, u32[]{:S(2)}, u32[]{:S(2)}) async-start(bf16[128,4,1024]{0,1,2:T(4,128)(2,1)} %copy.85), calls=%async_computation.2 | async-start | bytes 2097152 | tf_op jit(solution)/shard_map/all_to_all | solution.py:55
  249.9 28.7 %all-to-all-done.2 = bf16[128,4,1024]{0,1,2:T(4,128)(2,1)S(1)} async-done(((bf16[128,4,1024]{0,1,2:T(4,128)(2,1)}), bf16[128,4,1024]{0,1,2:T(4,128)(2,1)S(1)}, u32[]{:S(2)}, u32[]{:S(2)}) %all-to-all-start.2) | async-done | bytes 1048608 | tf_op jit(solution)/shard_map/all_to_all | solution.py:55
  284.7 1.7 copy.94
  286.3 5.0 all-to-all-start.3
  291.3 1.7 copy.96
  293.0 27.2 %all-to-all-done.3 = bf16[128,128,32]{1,2,0:T(8,128)(2,1)S(1)} async-done(((bf16[128,128,32]{1,2,0:T(8,128)(2,1)}), bf16[128,128,32]{1,2,0:T(8,128)(2,1)S(1)}, u32[]{:S(2)}, u32[]{:S(2)}) %all-to-all-start.3) | async-done | bytes 1048608 | tf_op jit(solution)/shard_map/all_to_all | solution.py:39
  320.2 5.0 all-to-all-start.4
  325.4 28.8 %all-to-all-done.4 = bf16[128,128,32]{1,2,0:T(8,128)(2,1)} async-done(((bf16[128,128,32]{1,2,0:T(8,128)(2,1)}), bf16[128,128,32]{1,2,0:T(8,128)(2,1)}, u32[]{:S(2)}, u32[]{:S(2)}) %all-to-all-start.4) | async-done | bytes 1048608 | tf_op jit(solution)/shard_map/all_to_all | solution.py:38
  355.6 5.6 %convert_bitcast_fusion = bf16[1024,4,1024]{0,2,1:T(8,128)(2,1)} fusion(bf16[4,128,1024]{1,2,0:T(8,128)(2,1)S(1)} %bitcast.125, bf16[4,128,1024]{1,2,0:T(8,128)(2,1)S(1)} %bitcast.126), kind=kOutput, calls=%fused_computation | convolution fusion | flops 1077936128 | bytes 10485760 | tf_op jit(solution)/shard_map/gki,gkj->igj/dot_general | solution.py:50
  361.2 79.6 %reduce-scatter.5.cloned.1.call-done = bf16[256,4,1024]{0,2,1:T(8,128)(2,1)} async-done(((bf16[1024,4,1024]{0,2,1:T(8,128)(2,1)}), bf16[256,4,1024]{0,2,1:T(8,128)(2,1)}) %reduce-scatter.5.cloned.1.call-update) | async-done | bytes 2097168 | tf_op jit(solution)/shard_map/reduce_scatter | solution.py:14
  440.8 4.1 copy.120
  445.0 36.6 %reduce-scatter.7.cloned.1.call-done = bf16[128,4096]{1,0:T(8,128)(2,1)} async-done(((bf16[256,4096]{1,0:T(8,128)(2,1)}), bf16[128,4096]{1,0:T(8,128)(2,1)}) %reduce-scatter.7.cloned.1.call-update) | async-done | bytes 1048592
  483.2 1.8 copy.99
  485.0 10.1 %all-to-all-start.5 = ((bf16[128,4,1024]{0,1,2:T(4,128)(2,1)}), bf16[128,4,1024]{0,1,2:T(4,128)(2,1)S(1)}, u32[]{:S(2)}, u32[]{:S(2)}) async-start(bf16[128,4,1024]{0,1,2:T(4,128)(2,1)} %copy.99), calls=%async_computation.6 | async-start | bytes 2097152 | tf_op jit(solution)/shard_map/all_to_all | solution.py:55
  495.3 1.9 fusion.55
  497.2 26.8 %all-to-all-done.5 = bf16[128,4,1024]{0,1,2:T(4,128)(2,1)S(1)} async-done(((bf16[128,4,1024]{0,1,2:T(4,128)(2,1)}), bf16[128,4,1024]{0,1,2:T(4,128)(2,1)S(1)}, u32[]{:S(2)}, u32[]{:S(2)}) %all-to-all-start.5) | async-done | bytes 1048608 | tf_op jit(solution)/shard_map/all_to_all | solution.py:55
  527.3 1.7 copy.105
  (61 shorter events, 18.3 us)
Async XLA Ops:
  6.5 2.6 copy-start.5
  6.5 2.6 copy-start.1
  6.5 225.8 %all-gather.2.cloned.1.call-start = ((), (), s32[]{:S(2)}) async-start(), calls=%async_computation.8 | async-start | bytes 9437184 | tf_op jit(solution)/shard_map/all_gather | solution.py:45
  238.1 11.6 %copy-start.6 = (f32[2,128]{1,0:T(2,128)S(1)}, f32[2,128]{1,0:T(2,128)}, u32[]{:S(2)}) copy-start(f32[2,128]{1,0:T(2,128)} %param.11) | copy-start | bytes 3076
  239.9 38.7 %all-to-all-start.2 = ((bf16[128,4,1024]{0,1,2:T(4,128)(2,1)}), bf16[128,4,1024]{0,1,2:T(4,128)(2,1)S(1)}, u32[]{:S(2)}, u32[]{:S(2)}) async-start(bf16[128,4,1024]{0,1,2:T(4,128)(2,1)} %copy.85), calls=%async_computation.2 | async-start | bytes 2097152 | tf_op jit(solution)/shard_map/all_to_all | solution.py:55
  279.2 0.8 copy-start.3
  279.8 0.9 copy-start.2
  286.3 33.9 %all-to-all-start.3 = ((bf16[128,128,32]{1,2,0:T(8,128)(2,1)}), bf16[128,128,32]{1,2,0:T(8,128)(2,1)S(1)}, u32[]{:S(2)}, u32[]{:S(2)}) async-start(bf16[128,128,32]{1,2,0:T(8,128)(2,1)} %copy.94), calls=%async_computation.3 | async-start | bytes 2097152 | tf_op jit(solution)/shard_map/all_to_all | solution.py:39
  320.2 34.0 %all-to-all-start.4 = ((bf16[128,128,32]{1,2,0:T(8,128)(2,1)}), bf16[128,128,32]{1,2,0:T(8,128)(2,1)}, u32[]{:S(2)}, u32[]{:S(2)}) async-start(bf16[128,128,32]{1,2,0:T(8,128)(2,1)} %copy.96), calls=%async_computation.4 | async-start | bytes 2097152 | tf_op jit(solution)/shard_map/all_to_all | solution.py:38
  325.3 115.5 %reduce-scatter.5.cloned.1.call-start = ((), (), s32[]{:S(2)}) async-start(), calls=%async_computation.9 | async-start | bytes 10485760 | tf_op jit(solution)/shard_map/reduce_scatter | solution.py:14
  361.2 120.4 %reduce-scatter.7.cloned.1.call-start = ((), (), s32[]{:S(2)}) async-start(), calls=%async_computation.10 | async-start | bytes 3145728
  485.0 39.0 %all-to-all-start.5 = ((bf16[128,4,1024]{0,1,2:T(4,128)(2,1)}), bf16[128,4,1024]{0,1,2:T(4,128)(2,1)S(1)}, u32[]{:S(2)}, u32[]{:S(2)}) async-start(bf16[128,4,1024]{0,1,2:T(4,128)(2,1)} %copy.99), calls=%async_computation.6 | async-start | bytes 2097152 | tf_op jit(solution)/shard_map/all_to_all | solution.py:55
  524.7 1.6 copy-start
  524.7 1.6 copy-start.4
Sparse Core Ops, SparseCore 0:
  55.4 176.9 all-gather.1
  361.3 79.5 reduce-scatter.4
  445.1 36.4 reduce-scatter.6
where the time goes:
time: 536 us; the launch traced here: 535 us
  waiting for transfers between devices  370 us (69%)
  blocking collectives  74.2 us (14%)
  starting transfers between devices  30 us (6%)
  local copies, waits for them, and re-layouts  24.2 us (5%)
  matrix products  18.5 us (3%)
  between operations  13.4 us (2%)
    all_gather x1, waiting for transfers between devices, local(): lax.all_gather(right_rows, ROW, axis=1, tiled=True)  142 us
    reduce_scatter x1, waiting for transfers between devices, sum_by_axis(): subtotal = lax.psum_scatter(subtotal, axis, scatter_dimension=0, tiled=True)  79.6 us
    all_to_all x2, waiting for transfers between devices, local(): lax.all_to_all(triangle.astype(jnp.bfloat16), 'col', split_axis=2, concat...  55.5 us
    all_to_all x1, blocking collectives, local(): lax.all_to_all(right_hand, 'col', split_axis=0, concat_axis=2, tiled=True)  40.5 us
    unnamed x4, waiting for transfers between devices  36.6 us
    all_to_all x1, blocking collectives, local(): lax.all_to_all(left_hand, 'col', split_axis=0, concat_axis=2, tiled=True)  33.7 us
    all_to_all x1, waiting for transfers between devices, local(): lax.all_to_all(left_hand, 'col', split_axis=0, concat_axis=2, tiled=True)  28.8 us
    all_to_all x1, waiting for transfers between devices, local(): lax.all_to_all(right_hand, 'col', split_axis=0, concat_axis=2, tiled=True)  27.2 us
  transfers between devices with their start and end apart: 7, of which 7 were waited for; matrix products, arithmetic and copies ran while one was open for 1% of the time, Pallas kernels for 0%

commit v1 on v0

--- a/solution.py
+++ b/solution.py
@@ -6,6 +6,11 @@
 
 ROW = ("row_0", "row_1")
 epsilon = 1e-05
+
+
+def swapped_in(value, axis, along):
+    outgoing = jnp.stack([value] * lax.axis_size(axis))
+    return jnp.concatenate(lax.all_to_all(outgoing, axis, 0, 0), axis=along)
 
 
 def sum_by_axis(terms, axes):
@@ -42,7 +47,7 @@
             triangle = jnp.einsum(
                 "gik,gjk->igj",
                 left_rows,
-                lax.all_gather(right_rows, ROW, axis=1, tiled=True),
+                swapped_in(right_rows, ROW, 1),
                 preferred_element_type=jnp.float32,
             )
         else:

time: 536 us -> 498 us (0.929)
  blocking collectives: 74.2 us -> 0 us
  starting transfers between devices: 30 us -> 47.4 us
  local copies, waits for them, and re-layouts: 24.2 us -> 38.6 us
    all_gather x1 -> x0, waiting for transfers between devices: 142 us -> none  [local(): lax.all_gather(right_rows, ROW, axis=1, tiled=True)]
    all_to_all x0 -> x1, waiting for transfers between devices: none -> 94.1 us  [swapped_in(): return jnp.concatenate(lax.all_to_all(outgoing, axis, 0, 0), axis=along)]
    all_to_all x2 -> x0, blocking collectives: 74.2 us -> none  [the longest x1 40.5 us: local(): lax.all_to_all(right_hand, 'col', split_axis=0, concat_axis=2, tiled=True)]
    all_to_all x1 -> x2, waiting for transfers between devices: 27.2 us -> 54.4 us  [local(): lax.all_to_all(right_hand, 'col', split_axis=0, concat_axis=2, tiled=True)]
    all_to_all x1 -> x2, waiting for transfers between devices: 28.8 us -> 55.2 us  [local(): lax.all_to_all(left_hand, 'col', split_axis=0, concat_axis=2, tiled=True)]
    all_to_all x1 -> x2, starting transfers between devices: 4.99 us -> 16.6 us  [local(): lax.all_to_all(right_hand, 'col', split_axis=0, concat_axis=2, tiled=True)]
    reshape x0 -> x1, local copies, waits for them, and re-layouts: none -> 8.18 us  [swapped_in(): return jnp.concatenate(lax.all_to_all(outgoing, axis, 0, 0), axis=along)]
    another operation x0 -> x2, local copies, waits for them, and re-layouts: none -> 5.78 us  [swapped_in(): outgoing = jnp.stack([value] * lax.axis_size(axis))]
  transfers between devices with their start and end apart: 7 -> 9, of which waited for: 7 -> 9; matrix products, arithmetic and copies ran while one was open for 1% -> 2% of each run, Pallas kernels for 0% -> 0%
where the time goes in v1:
time: 498 us; the launch traced here: 497 us
  waiting for transfers between devices  374 us (75%)
  starting transfers between devices  47.4 us (10%)
  local copies, waits for them, and re-layouts  38.6 us (8%)
  matrix products  18.5 us (4%)
  between operations  13.7 us (3%)
  other arithmetic  4.98 us (1%)
    all_to_all x1, waiting for transfers between devices, swapped_in(): return jnp.concatenate(lax.all_to_all(outgoing, axis, 0, 0), axis=along)  94.1 us
    reduce_scatter x1, waiting for transfers between devices, sum_by_axis(): subtotal = lax.psum_scatter(subtotal, axis, scatter_dimension=0, tiled=True)  77.8 us
    all_to_all x2, waiting for transfers between devices, local(): lax.all_to_all(triangle.astype(jnp.bfloat16), 'col', split_axis=2, concat...  55.5 us
    all_to_all x2, waiting for transfers between devices, local(): lax.all_to_all(left_hand, 'col', split_axis=0, concat_axis=2, tiled=True)  55.2 us
    all_to_all x2, waiting for transfers between devices, local(): lax.all_to_all(right_hand, 'col', split_axis=0, concat_axis=2, tiled=True)  54.4 us
    unnamed x3, waiting for transfers between devices  36.6 us
    all_to_all x2, starting transfers between devices, local(): lax.all_to_all(right_hand, 'col', split_axis=0, concat_axis=2, tiled=True)  16.6 us
    all_to_all x2, starting transfers between devices, local(): lax.all_to_all(triangle.astype(jnp.bfloat16), 'col', split_axis=2, concat...  15.6 us
  transfers between devices with their start and end apart: 9, of which 9 were waited for; matrix products, arithmetic and copies ran while one was open for 2% of the time, Pallas kernels for 0%

profile of v1, /device:TPU:4, one launch (start us, length us, event | category | flops | bytes accessed | tf_op | source)
XLA Modules:
  0.0 496.8 jit_solution(4690677529215169085)
XLA Ops:
  6.5 2.0 copy.75
  13.3 11.6 %all-to-all-start = ((bf16[128,128,32]{1,2,0:T(8,128)(2,1)}), bf16[128,128,32]{1,2,0:T(8,128)(2,1)S(1)}, u32[]{:S(2)}, u32[]{:S(2)}) async-start(bf16[128,128,32]{1,2,0:T(8,128)(2,1)} %copy.79), calls=%async_computation | async-start | bytes 2097152 | tf_op jit(solution)/shard_map/all_to_all | solution.py:44
  26.6 27.2 %all-to-all-done = bf16[128,128,32]{1,2,0:T(8,128)(2,1)S(1)} async-done(((bf16[128,128,32]{1,2,0:T(8,128)(2,1)}), bf16[128,128,32]{1,2,0:T(8,128)(2,1)S(1)}, u32[]{:S(2)}, u32[]{:S(2)}) %all-to-all-start) | async-done | bytes 1048608 | tf_op jit(solution)/shard_map/all_to_all | solution.py:44
  53.8 5.0 %all-to-all-start.2 = ((bf16[128,128,32]{1,2,0:T(8,128)(2,1)}), bf16[128,128,32]{1,2,0:T(8,128)(2,1)S(1)}, u32[]{:S(2)}, u32[]{:S(2)}) async-start(bf16[128,128,32]{1,2,0:T(8,128)(2,1)} %copy.83), calls=%async_computation.2 | async-start | bytes 2097152 | tf_op jit(solution)/shard_map/all_to_all | solution.py:43
  61.4 26.4 %all-to-all-done.2 = bf16[128,128,32]{1,2,0:T(8,128)(2,1)S(1)} async-done(((bf16[128,128,32]{1,2,0:T(8,128)(2,1)}), bf16[128,128,32]{1,2,0:T(8,128)(2,1)S(1)}, u32[]{:S(2)}, u32[]{:S(2)}) %all-to-all-start.2) | async-done | bytes 1048608 | tf_op jit(solution)/shard_map/all_to_all | solution.py:43
  87.7 4.3 stack.5
  92.0 5.1 %all-to-all-start.1 = ((bf16[8,4,128,1024]{3,2,1,0:T(8,128)(2,1)}), bf16[8,4,128,1024]{3,2,1,0:T(8,128)(2,1)}, u32[]{:S(2)}, u32[]{:S(2)}) async-start(bf16[8,4,128,1024]{3,2,1,0:T(8,128)(2,1)} %stack.5), calls=%async_computation.1 | async-start | bytes 16777216 | tf_op jit(solution)/shard_map/all_to_all | solution.py:13
  97.2 94.1 %all-to-all-done.1 = bf16[8,4,128,1024]{3,2,1,0:T(8,128)(2,1)} async-done(((bf16[8,4,128,1024]{3,2,1,0:T(8,128)(2,1)}), bf16[8,4,128,1024]{3,2,1,0:T(8,128)(2,1)}, u32[]{:S(2)}, u32[]{:S(2)}) %all-to-all-start.1) | async-done | bytes 8388640 | tf_op jit(solution)/shard_map/all_to_all | solution.py:13
  191.3 8.2 %copy.82 = bf16[4,8,128,1024]{3,2,1,0:T(8,128)(2,1)} copy(bf16[4,8,128,1024]{3,2,0,1:T(8,128)(2,1)} %bitcast.11) | data formatting | bytes 16777216 | tf_op jit(solution)/shard_map/reshape | solution.py:13
  199.5 5.7 %fusion.42 = bf16[128,4,1024]{0,2,1:T(8,128)(2,1)S(1)} fusion(bf16[4,1024,1024]{2,1,0:T(8,128)(2,1)} %bitcast.127, bf16[4,128,1024]{1,2,0:T(8,128)(2,1)S(1)} %bitcast.137), kind=kOutput, calls=%fused_computation.62 | convolution fusion | flops 1074266112 | bytes 10485760 | tf_op jit(solution)/shard_map/gik,gjk->igj/dot_general | solution.py:47
  205.2 1.8 copy.86
  207.0 5.5 %all-to-all-start.3 = ((bf16[128,4,1024]{0,1,2:T(4,128)(2,1)}), bf16[128,4,1024]{0,1,2:T(4,128)(2,1)S(1)}, u32[]{:S(2)}, u32[]{:S(2)}) async-start(bf16[128,4,1024]{0,1,2:T(4,128)(2,1)} %copy.86), calls=%async_computation.3 | async-start | bytes 2097152 | tf_op jit(solution)/shard_map/all_to_all | solution.py:60
  212.7 28.7 %all-to-all-done.3 = bf16[128,4,1024]{0,1,2:T(4,128)(2,1)S(1)} async-done(((bf16[128,4,1024]{0,1,2:T(4,128)(2,1)}), bf16[128,4,1024]{0,1,2:T(4,128)(2,1)S(1)}, u32[]{:S(2)}, u32[]{:S(2)}) %all-to-all-start.3) | async-done | bytes 1048608 | tf_op jit(solution)/shard_map/all_to_all | solution.py:60
  249.1 5.0 %all-to-all-start.4 = ((bf16[128,128,32]{1,2,0:T(8,128)(2,1)}), bf16[128,128,32]{1,2,0:T(8,128)(2,1)S(1)}, u32[]{:S(2)}, u32[]{:S(2)}) async-start(bf16[128,128,32]{1,2,0:T(8,128)(2,1)} %copy.95), calls=%async_computation.4 | async-start | bytes 2097152 | tf_op jit(solution)/shard_map/all_to_all | solution.py:44
  255.8 27.2 %all-to-all-done.4 = bf16[128,128,32]{1,2,0:T(8,128)(2,1)S(1)} async-done(((bf16[128,128,32]{1,2,0:T(8,128)(2,1)}), bf16[128,128,32]{1,2,0:T(8,128)(2,1)S(1)}, u32[]{:S(2)}, u32[]{:S(2)}) %all-to-all-start.4) | async-done | bytes 1048608 | tf_op jit(solution)/shard_map/all_to_all | solution.py:44
  283.0 5.0 %all-to-all-start.5 = ((bf16[128,128,32]{1,2,0:T(8,128)(2,1)}), bf16[128,128,32]{1,2,0:T(8,128)(2,1)}, u32[]{:S(2)}, u32[]{:S(2)}) async-start(bf16[128,128,32]{1,2,0:T(8,128)(2,1)} %copy.97), calls=%async_computation.5 | async-start | bytes 2097152 | tf_op jit(solution)/shard_map/all_to_all | solution.py:43
  288.2 28.8 %all-to-all-done.5 = bf16[128,128,32]{1,2,0:T(8,128)(2,1)} async-done(((bf16[128,128,32]{1,2,0:T(8,128)(2,1)}), bf16[128,128,32]{1,2,0:T(8,128)(2,1)}, u32[]{:S(2)}, u32[]{:S(2)}) %all-to-all-start.5) | async-done | bytes 1048608 | tf_op jit(solution)/shard_map/all_to_all | solution.py:43
  318.4 5.6 %convert_bitcast_fusion = bf16[1024,4,1024]{0,2,1:T(8,128)(2,1)} fusion(bf16[4,128,1024]{1,2,0:T(8,128)(2,1)S(1)} %bitcast.128, bf16[4,128,1024]{1,2,0:T(8,128)(2,1)S(1)} %bitcast.129), kind=kOutput, calls=%fused_computation | convolution fusion | flops 1077936128 | bytes 10485760 | tf_op jit(solution)/shard_map/gki,gkj->igj/dot_general | solution.py:55
  324.0 77.8 %reduce-scatter.5.cloned.1.call-done = bf16[256,4,1024]{0,2,1:T(8,128)(2,1)} async-done(((bf16[1024,4,1024]{0,2,1:T(8,128)(2,1)}), bf16[256,4,1024]{0,2,1:T(8,128)(2,1)}) %reduce-scatter.5.cloned.1.call-update) | async-done | bytes 2097168 | tf_op jit(solution)/shard_map/reduce_scatter | solution.py:19
  401.9 4.1 copy.121
  406.0 36.6 %reduce-scatter.7.cloned.1.call-done = bf16[128,4096]{1,0:T(8,128)(2,1)} async-done(((bf16[256,4096]{1,0:T(8,128)(2,1)}), bf16[128,4096]{1,0:T(8,128)(2,1)}) %reduce-scatter.7.cloned.1.call-update) | async-done | bytes 1048592
  446.0 10.1 %all-to-all-start.6 = ((bf16[128,4,1024]{0,1,2:T(4,128)(2,1)}), bf16[128,4,1024]{0,1,2:T(4,128)(2,1)S(1)}, u32[]{:S(2)}, u32[]{:S(2)}) async-start(bf16[128,4,1024]{0,1,2:T(4,128)(2,1)} %copy.100), calls=%async_computation.7 | async-start | bytes 2097152 | tf_op jit(solution)/shard_map/all_to_all | solution.py:60
  456.3 1.9 fusion.55
  458.2 26.8 %all-to-all-done.6 = bf16[128,4,1024]{0,1,2:T(4,128)(2,1)S(1)} async-done(((bf16[128,4,1024]{0,1,2:T(4,128)(2,1)}), bf16[128,4,1024]{0,1,2:T(4,128)(2,1)S(1)}, u32[]{:S(2)}, u32[]{:S(2)}) %all-to-all-start.6) | async-done | bytes 1048608 | tf_op jit(solution)/shard_map/all_to_all | solution.py:60
  (64 shorter events, 28.7 us)
Async XLA Ops:
  6.5 2.6 copy-start.5
  6.5 2.6 copy-start.1
  13.3 40.5 %all-to-all-start = ((bf16[128,128,32]{1,2,0:T(8,128)(2,1)}), bf16[128,128,32]{1,2,0:T(8,128)(2,1)S(1)}, u32[]{:S(2)}, u32[]{:S(2)}) async-start(bf16[128,128,32]{1,2,0:T(8,128)(2,1)} %copy.79), calls=%async_computation | async-start | bytes 2097152 | tf_op jit(solution)/shard_map/all_to_all | solution.py:44
  53.8 33.9 %all-to-all-start.2 = ((bf16[128,128,32]{1,2,0:T(8,128)(2,1)}), bf16[128,128,32]{1,2,0:T(8,128)(2,1)S(1)}, u32[]{:S(2)}, u32[]{:S(2)}) async-start(bf16[128,128,32]{1,2,0:T(8,128)(2,1)} %copy.83), calls=%async_computation.2 | async-start | bytes 2097152 | tf_op jit(solution)/shard_map/all_to_all | solution.py:43
  92.0 99.3 %all-to-all-start.1 = ((bf16[8,4,128,1024]{3,2,1,0:T(8,128)(2,1)}), bf16[8,4,128,1024]{3,2,1,0:T(8,128)(2,1)}, u32[]{:S(2)}, u32[]{:S(2)}) async-start(bf16[8,4,128,1024]{3,2,1,0:T(8,128)(2,1)} %stack.5), calls=%async_computation.1 | async-start | bytes 16777216 | tf_op jit(solution)/shard_map/all_to_all | solution.py:13
  205.2 7.3 %copy-start.6 = (f32[2,128]{1,0:T(2,128)S(1)}, f32[2,128]{1,0:T(2,128)}, u32[]{:S(2)}) copy-start(f32[2,128]{1,0:T(2,128)} %param.11) | copy-start | bytes 3076
  207.0 34.4 %all-to-all-start.3 = ((bf16[128,4,1024]{0,1,2:T(4,128)(2,1)}), bf16[128,4,1024]{0,1,2:T(4,128)(2,1)S(1)}, u32[]{:S(2)}, u32[]{:S(2)}) async-start(bf16[128,4,1024]{0,1,2:T(4,128)(2,1)} %copy.86), calls=%async_computation.3 | async-start | bytes 2097152 | tf_op jit(solution)/shard_map/all_to_all | solution.py:60
  242.0 0.8 copy-start.3
  242.5 0.9 copy-start.2
  249.1 33.9 %all-to-all-start.4 = ((bf16[128,128,32]{1,2,0:T(8,128)(2,1)}), bf16[128,128,32]{1,2,0:T(8,128)(2,1)S(1)}, u32[]{:S(2)}, u32[]{:S(2)}) async-start(bf16[128,128,32]{1,2,0:T(8,128)(2,1)} %copy.95), calls=%async_computation.4 | async-start | bytes 2097152 | tf_op jit(solution)/shard_map/all_to_all | solution.py:44
  283.0 34.0 %all-to-all-start.5 = ((bf16[128,128,32]{1,2,0:T(8,128)(2,1)}), bf16[128,128,32]{1,2,0:T(8,128)(2,1)}, u32[]{:S(2)}, u32[]{:S(2)}) async-start(bf16[128,128,32]{1,2,0:T(8,128)(2,1)} %copy.97), calls=%async_computation.5 | async-start | bytes 2097152 | tf_op jit(solution)/shard_map/all_to_all | solution.py:43
  288.1 113.8 %reduce-scatter.5.cloned.1.call-start = ((), (), s32[]{:S(2)}) async-start(), calls=%async_computation.9 | async-start | bytes 10485760 | tf_op jit(solution)/shard_map/reduce_scatter | solution.py:19
  324.0 118.6 %reduce-scatter.7.cloned.1.call-start = ((), (), s32[]{:S(2)}) async-start(), calls=%async_computation.10 | async-start | bytes 3145728
  446.0 39.0 %all-to-all-start.6 = ((bf16[128,4,1024]{0,1,2:T(4,128)(2,1)}), bf16[128,4,1024]{0,1,2:T(4,128)(2,1)S(1)}, u32[]{:S(2)}, u32[]{:S(2)}) async-start(bf16[128,4,1024]{0,1,2:T(4,128)(2,1)} %copy.100), calls=%async_computation.7 | async-start | bytes 2097152 | tf_op jit(solution)/shard_map/all_to_all | solution.py:60
  485.7 1.6 copy-start
  485.7 1.6 copy-start.4
Sparse Core Ops, SparseCore 0:
  324.1 77.7 reduce-scatter.4
  406.1 36.4 reduce-scatter.6
